TPU v7x, 32 devices: a whole 2x2x4 slice. The times are simulated.
32 devices in a mesh: groups: 2 (over y), range: 8 (over z, x), sub: 2 (over core).
Axes of the slice: x: 2, y: 2, z: 4, core: 2. Of those that a mesh axis runs over, the one named last changes fastest.
Arguments:
- samples: float32 [2, 1024, 32, 128], P(None, ('groups', 'range', 'sub')), parts along dimension 1, may hold values from -6 to 6
- beam_weights: float32 [32, 8, 2, 64, 128], P(('groups', 'range'), None, None, None, 'sub'), parts along dimension 0, may hold values from -0.25 to 0.25
- subarrays: int32 [32, 8, 64], P(('groups', 'range', 'sub')), parts along dimension 0, may hold values from 0 to 511, as said below
- training: int32 [64], P(('groups', 'range', 'sub')), parts along dimension 0, may hold values 0 or 1
Outputs:
- covariance: float32 [32, 8, 64, 128], P(('groups', 'range', 'sub')), parts along dimension 0
- filtered: float32 [2, 128, 64, 128], P(None, None, ('groups', 'range', 'sub')), parts along dimension 2
- energy: float32 [256], P('groups'), parts along dimension 0
There are 2 independent parts, one for each index of `groups`. A program takes and returns all parts, laid end to end along the dimension named above; each array names one. Nothing has to cross between parts.
Inputs may be any that keep to these rules, and one draw needn't show every extreme that they name: `subarrays`: in each gate block the 512 indices are all 512 channels, each once.
All inputs are finite; a program needn't handle non-finite values. No bound on the sum of `training` on one device may be relied on, other than what follows from the above.
Results may differ from a plain program's by a relative error of at most 0.0003.
Values sent between devices are 32-bit elements; how exact they have to be, the bound alone decides.
A program may use at most 64 MiB of HBM per device.

v0:
```python
import functools

import jax
import jax.numpy as jnp
from jax import lax
from jax.experimental import pallas as pl
from jax.experimental.pallas import tpu as pltpu
from jax.sharding import PartitionSpec as P

GB = 2
loading = 0.05
F32 = jnp.float32
BF16 = jnp.bfloat16


def split(x):
    hi = x.astype(BF16)
    return hi, (x - hi.astype(F32)).astype(BF16)


def dot(a, b):
    return jnp.dot(a, b, preferred_element_type=F32)


def dot_t(a, b):
    return lax.dot_general(a, b, (((1,), (1,)), ((), ())), preferred_element_type=F32)


def partner(me, step, count):
    other, bit = me, 1
    while bit < count:
        other = other + ((step // bit) % 2) * (1 - 2 * ((me // bit) % 2)) * bit
        bit *= 2
    return other


def kernel(
    dims,
    smp, bw, sub_in, trn_in,
    cov, filt, en,
    sub, trn, stage, sendb, recv, wfull, lhs, wst, wq, sacc, gacc, esend, erecv,
    send_sem, recv_sem, wsem, esend_sem, erecv_sem, lsem,
):
    n, cores, c_loc, gates, pulses, ns, s_n, k_half = dims
    beams = 2 * k_half
    chans = n * c_loc
    part = n // 4
    rows = part * c_loc
    core = lax.axis_index("sub")
    me = lax.axis_index("range") * cores + core

    def where(d):
        return {"range": d // cores, "sub": d % cores}

    barrier = pltpu.get_barrier_semaphore()

    def greet(t, c):
        pl.semaphore_signal(
            barrier,
            inc=1,
            device_id=where(partner(me, n - t, n)),
            device_id_type=pl.DeviceIdType.MESH,
        )
        return c

    lax.fori_loop(1, n, greet, 0)
    load = pltpu.make_async_copy(smp, stage, lsem.at[0])
    load.start()
    keep = pltpu.make_async_copy(bw.at[core], wfull.at[core], lsem.at[1])
    keep.start()

    small = [
        pltpu.make_async_copy(sub_in, sub, lsem.at[2]),
        pltpu.make_async_copy(trn_in, trn, lsem.at[3]),
    ]
    for copy in small:
        copy.start()
    load.wait()

    def arrange(d, c):
        for g in range(GB):
            sendb[d, g * 2 * c_loc : (g + 1) * 2 * c_loc, :] = stage[
                pl.ds(d * GB + g, 2 * c_loc, stride=gates), :
            ]
        return c

    lax.fori_loop(0, n, arrange, 0)
    recv[me] = sendb[me]
    pl.semaphore_wait(barrier, n - 1)

    def piece(d, slot, dev):
        return pltpu.make_async_remote_copy(
            src_ref=sendb.at[d],
            dst_ref=recv.at[slot],
            send_sem=send_sem.at[d],
            recv_sem=recv_sem.at[slot],
            device_id=where(dev),
            device_id_type=pl.DeviceIdType.MESH,
        )

    def launch(t, c):
        d = partner(me, t, n)
        piece(d, me, d).start()
        return c

    lax.fori_loop(n // 2, n, launch, 0)
    lax.fori_loop(1, n // 2, launch, 0)
    swap = pltpu.make_async_remote_copy(
        src_ref=bw.at[1 - core],
        dst_ref=wfull.at[core],
        send_sem=wsem.at[0],
        recv_sem=wsem.at[1],
        device_id={"sub": 1 - core},
        device_id_type=pl.DeviceIdType.MESH,
    )
    swap.start()

    for copy in small:
        copy.wait()
    keep.wait()
    swap.wait()
    chosen = jnp.concatenate([sub[s : s + 1, :] for s in range(ns)], axis=1)
    sides = []
    for iq in range(2):
        cols = []
        for s in range(ns):
            cols.append(
                jnp.concatenate([jnp.transpose(wfull[h, s, iq]) for h in range(2)], axis=0)
            )
        sides.append(cols)
    for s in range(ns):
        w_r, w_i = sides[0][s], sides[1][s]
        top = jnp.concatenate([w_r, -w_i], axis=1)
        low = jnp.concatenate([w_i, w_r], axis=1)
        wq[s] = jnp.concatenate([top, low], axis=0)
        hi, lo = split(jnp.concatenate([w_r, w_i], axis=0))
        wst[s, 0] = hi
        wst[s, 1] = lo
    flat = jnp.concatenate([jnp.concatenate(cols, axis=1) for cols in sides], axis=0)
    w_hi, w_lo = split(flat)
    for ch in range(4):
        r = lax.broadcasted_iota(jnp.int32, (rows, chans), 0)
        if c_loc % 8 == 0:
            chan = r + ch * rows
        else:
            chan = (ch * part + r % part) * c_loc + r // part
        pick = jnp.where(chan == chosen, 1.0, 0.0).astype(F32)
        pick_b = pick.astype(BF16)
        lhs[ch, 0:chans, :] = jnp.transpose(pick).astype(BF16)
        lhs[ch, chans : chans + 2 * beams, :] = dot_t(w_hi, pick_b).astype(BF16)
        lhs[ch, chans + 2 * beams : chans + 4 * beams, :] = dot_t(w_lo, pick_b).astype(BF16)

    lanes = GB * pulses
    e_re = e_im = None
    for q in (0, 1, 2, 3):
        ch = partner(me // part, q, 4)

        def arrive(t, c):
            src = partner(me, t, n)
            piece(src, src, src).wait_recv()
            return c

        lax.fori_loop(max(1, q * part), (q + 1) * part, arrive, 0)
        parts = []
        for iq in range(2):
            for g in range(GB):
                j = (g * 2 + iq) * c_loc
                if c_loc % 8 == 0:
                    block = recv[pl.ds(ch * part, part), j : j + c_loc, :].reshape(rows, pulses)
                else:
                    block = jnp.concatenate(
                        [
                            recv[pl.ds(ch * part, part), j + c : j + c + 1, :].reshape(part, pulses)
                            for c in range(c_loc)
                        ],
                        axis=0,
                    )
                parts.append(block)
        z = jnp.concatenate(parts, axis=1)
        z_hi, z_lo = split(z)
        l_hi = lhs[ch, chans : chans + 2 * beams, :]
        l_lo = lhs[ch, chans + 2 * beams : chans + 4 * beams, :]
        term = dot(l_hi, z_hi) + (dot(l_hi, z_lo) + dot(l_lo, z_hi))
        if q == 0:
            sacc[...] = term
        elif q != 3:
            sacc[...] = sacc[...] + term
        else:
            full = sacc[...] + term
            e_re = full[:beams, :lanes] + full[beams:, lanes:]
            e_im = full[:beams, lanes:] - full[beams:, :lanes]
            p_hi, p_lo = split(e_re * e_re + e_im * e_im)
            ones = jnp.ones((8, lanes), BF16)
            esum = (dot_t(ones, p_hi) + dot_t(ones, p_lo))[0:1]
            esend[...] = esum
            erecv[me] = esum

            def share(t, c):
                d = partner(me, n - t, n)
                report(d, me, d).start()
                return c

            def report(d, slot, dev):
                return pltpu.make_async_remote_copy(
                    src_ref=esend,
                    dst_ref=erecv.at[slot],
                    send_sem=esend_sem.at[d],
                    recv_sem=erecv_sem.at[slot],
                    device_id=where(dev),
                    device_id_type=pl.DeviceIdType.MESH,
                )

            lax.fori_loop(1, n, share, 0)
        sel = lhs[ch, 0:chans, :]
        g_hi, g_lo = dot(sel, z_hi), dot(sel, z_lo)
        if q == 0:
            gacc[0] = g_hi
            gacc[1] = g_lo
        else:
            gacc[0] = gacc[0] + g_hi
            gacc[1] = gacc[1] + g_lo

    factor = 1.0 / lanes
    lane = lax.broadcasted_iota(jnp.int32, (1, 2 * lanes), 1)
    first = trn[0].astype(F32)
    second = trn[1].astype(F32)
    gate = (lane // pulses) % GB
    mask = jnp.where(gate == 0, first, second)
    power = jnp.zeros((beams, 2 * s_n), F32)
    for s in range(ns):
        x = [gacc[i, s * s_n : (s + 1) * s_n, :] for i in range(2)]
        left = [(v * mask).astype(BF16) for v in x]
        right = [
            jnp.concatenate(
                [v, jnp.concatenate([-v[:, lanes:], v[:, :lanes]], axis=1)], axis=0
            ).astype(BF16)
            for v in x
        ]
        r_s = (
            dot_t(left[0], right[0]) + (dot_t(left[0], right[1]) + dot_t(left[1], right[0]))
        ) * factor
        cov[s] = r_s
        r_hi, r_lo = split(r_s)
        w_h, w_l = wst[s, 0], wst[s, 1]
        t_s = (dot(w_h, r_hi) + (dot(w_h, r_lo) + dot(w_l, r_hi))) * wq[s]
        power = power + t_s[:beams] + t_s[beams:]
    quadratic = jnp.sum(power, axis=1, keepdims=True)
    inverse = 1.0 / jnp.sqrt(quadratic + loading)
    for g in range(GB):
        filt[0, pl.ds(g, beams, stride=GB), :] = e_re[:, g * pulses : (g + 1) * pulses] * inverse
        filt[1, pl.ds(g, beams, stride=GB), :] = e_im[:, g * pulses : (g + 1) * pulses] * inverse

    def close(t, c):
        d = partner(me, t, n)
        report(d, d, d).wait_recv()
        report(d, d, d).wait_send()
        piece(d, d, d).wait_send()
        return c

    lax.fori_loop(1, n, close, 0)
    total = jnp.sum(erecv[...], axis=0)
    en[...] = total * (1.0 / (gates * pulses))


def store(cov, filt, en, cov_out, filt_out, en_out, sem):
    pairs = ((cov, cov_out), (filt, filt_out), (en, en_out))
    copies = [pltpu.make_async_copy(a, b, sem.at[i]) for i, (a, b) in enumerate(pairs)]
    for copy in copies:
        copy.start()
    for copy in copies:
        copy.wait()


def body(samples, beam_weights, subarrays, training):
    range_count = lax.axis_size("range")
    cores = lax.axis_size("sub")
    n = range_count * cores
    parts_iq, c_loc, gates, pulses = samples.shape
    blocks, ns, _, s_n, k_half = beam_weights.shape
    assert gates == GB * n and blocks == cores == 2 and subarrays.shape[0] == 1
    assert n & (n - 1) == 0
    assert parts_iq == 2 and n * c_loc == ns * s_n
    beams, chans, lanes = 2 * k_half, n * c_loc, GB * pulses
    dims = (n, cores, c_loc, gates, pulses, ns, s_n, k_half)
    hbm = pl.BlockSpec(memory_space=pl.ANY)
    vmem = pl.BlockSpec(memory_space=pltpu.VMEM)
    dma = pltpu.SemaphoreType.DMA
    cov, filt, en = pl.pallas_call(
        functools.partial(kernel, dims),
        out_shape=(
            pltpu.VMEM((ns, s_n, 2 * s_n), F32),
            pltpu.VMEM((2, beams * GB, pulses), F32),
            pltpu.VMEM((1, beams), F32),
        ),
        in_specs=[hbm] * 4,
        out_specs=(vmem, vmem, vmem),
        scratch_shapes=[
            pltpu.VMEM((ns, s_n), jnp.int32),
            pltpu.SMEM((GB,), jnp.int32),
            pltpu.VMEM((2 * c_loc * gates, pulses), F32),
            pltpu.VMEM((n, 2 * GB * c_loc, pulses), F32),
            pltpu.VMEM((n, 2 * GB * c_loc, pulses), F32),
            pltpu.VMEM((2, ns, 2, s_n, k_half), F32),
            pltpu.VMEM((4, chans + 4 * beams, chans // 4), BF16),
            pltpu.VMEM((ns, 2, 2 * beams, s_n), BF16),
            pltpu.VMEM((ns, 2 * beams, 2 * s_n), F32),
            pltpu.VMEM((2 * beams, 2 * lanes), F32),
            pltpu.VMEM((2, chans, 2 * lanes), F32),
            pltpu.VMEM((1, beams), F32),
            pltpu.VMEM((n, 1, beams), F32),
            dma((n,)),
            dma((n,)),
            dma((2,)),
            dma((n,)),
            dma((n,)),
            dma((4,)),
        ],
        compiler_params=pltpu.CompilerParams(collective_id=0, has_side_effects=True),
    )(
        samples.reshape(2 * c_loc * gates, pulses),
        beam_weights,
        subarrays.reshape(ns, s_n),
        training,
    )
    cov, filt, en = (pltpu.with_memory_space_constraint(v, pltpu.VMEM) for v in (cov, filt, en))
    cov, filt, en = pl.pallas_call(
        store,
        out_shape=[jax.ShapeDtypeStruct(v.shape, F32) for v in (cov, filt, en)],
        in_specs=[vmem] * 3,
        out_specs=[hbm] * 3,
        scratch_shapes=[dma((3,))],
    )(cov, filt, en)
    return (
        cov.reshape(1, ns, s_n, 2 * s_n),
        filt.reshape(2, beams, GB, pulses),
        en.reshape(beams),
    )


def solution(mesh):
    placed = (
        P(None, ("groups", "range", "sub"), None, None),
        P(("groups", "range"), None, None, None, "sub"),
        P(("groups", "range", "sub"), None, None),
        P(("groups", "range", "sub")),
    )
    return jax.shard_map(
        body,
        mesh=mesh,
        in_specs=placed,
        out_specs=(
            P(("groups", "range", "sub"), None, None, None),
            P(None, None, ("groups", "range", "sub"), None),
            P("groups"),
        ),
        check_vma=False,
    )
```

profile of v0, /device:TPU:0, one launch (start us, length us, event | category | flops | bytes accessed | tf_op | source)
XLA Modules:
  0.0 36.6 jit_solution(2844402101704460924)
XLA Ops:
  0.6 35.2 %shard_map.67 = (f32[8,64,128]{2,1,0:T(8,128)S(1)}, f32[2,256,128]{2,1,0:T(8,128)S(1)}, f32[1,128]{1,0:T(1,128)S(1)}) custom-call(f32[2048,128]{1,0:T(8,128)} %bitcast.5, f32[2,8,2,64,64]{4,3,2,1,0:T(8,128)} %bw.1, s32[8,64]{1,0:T(8,128)} %bitcast.6, s32[2]{0:T(128)} %trn_in.1), custom_call_target="tpu_custom_call" | custom-call | tf_op jit(solution)/shard_map/pallas_call | solution.py:288
  35.8 0.8 %shard_map.68 = (f32[8,64,128]{2,1,0:T(8,128)}, f32[2,256,128]{2,1,0:T(8,128)}, f32[1,128]{1,0:T(1,128)}) custom-call(f32[8,64,128]{2,1,0:T(8,128)S(1)} %get-tuple-element.9.cov, f32[2,256,128]{2,1,0:T(8,128)S(1)} %get-tuple-element.10.filt, f32[1,128]{1,0:T(1,128)S(1)} %get-tuple-element.11.en), custom_call_target="tpu_custom_call" | custom-call | tf_op jit(solution)/shard_map/pallas_call | solution.py:326
where the time goes:
time: 36.8 us; the launch traced here: 36.6 us
  Pallas kernels  36 us (98%)
  between operations  0.64 us (2%)
    pallas_call x1, Pallas kernels, body(): pl.pallas_call(functools.partial(kernel, dims), out_shape=(pltpu.VMEM((ns...  35.2 us
    pallas_call x1, Pallas kernels, body(): pl.pallas_call(store, out_shape=[jax.ShapeDtypeStruct(v.shape, F32) for v...  0.82 us

commit v1 on v0

v1 whole, which is shorter than its diff:
```python
import functools

import jax
import jax.numpy as jnp
from jax import lax
from jax.experimental import pallas as pl
from jax.experimental.pallas import tpu as pltpu
from jax.sharding import PartitionSpec as P

GB = 2
loading = 0.05
F32 = jnp.float32
BF16 = jnp.bfloat16
MESH = pl.DeviceIdType.MESH


def split(x):
    hi = x.astype(BF16)
    return hi, (x - hi.astype(F32)).astype(BF16)


def dot(a, b):
    return jnp.dot(a, b, preferred_element_type=F32)


def dot_t(a, b):
    return lax.dot_general(a, b, (((1,), (1,)), ((), ())), preferred_element_type=F32)


def each(count, fn, first=0):
    if count - first <= 8:
        for i in range(first, count):
            fn(i)
    else:

        def step(i, c):
            fn(i)
            return c

        lax.fori_loop(first, count, step, 0)


def kernel(
    dims,
    smp, bw, sub_in, trn_in,
    cov, filt, en,
    sub, trn, sendb, recv, wfull, sel, wl, bq, wv, eacc, gat, ev, psum, esend, erecv,
    send_sem, recv_sem, fsem, wsem, esem, lsem,
):
    n, cores, c_loc, gates, pulses, ns, s_n, k_half = dims
    beams = 2 * k_half
    chans = n * c_loc
    part, half = n // 4, n // 2
    rows = half * c_loc
    core = lax.axis_index("sub")
    me = lax.axis_index("range") * cores + core
    plane, low = me // part, me % part
    upper = plane // 2
    planes = (3 - 3 * upper, 2 - upper, plane + 1 - 2 * (plane % 2), plane)

    def where(d):
        return {"range": d // cores, "sub": d % cores}

    def device(p, i):
        return planes[p] * part + (low + i) % part

    def slots(ref, g, p, count=None):
        return ref.at[g, pl.ds(planes[p] * part, count or part)]

    def fetch(d, g, p, ref):
        return pltpu.make_async_copy(smp.at[:, d * GB + g], ref.at[g, d], fsem.at[g, p])

    def piece(d, g, p):
        return pltpu.make_async_remote_copy(
            src_ref=sendb.at[g, d],
            dst_ref=recv.at[g, me],
            send_sem=send_sem.at[0],
            recv_sem=recv_sem.at[g, p],
            device_id=where(d),
            device_id_type=MESH,
        )

    def arrived(src, dst, p, g):
        return pltpu.make_async_remote_copy(
            src_ref=src,
            dst_ref=dst,
            send_sem=send_sem.at[0],
            recv_sem=recv_sem.at[g, p],
            device_id=where(device(2, 0)),
            device_id_type=MESH,
        )

    groups = [(g, p) for g in range(GB) for p in (0, 1)] + [(g, p) for g in range(GB) for p in (2, 3)]
    for g, p in groups:
        each(part, lambda i: fetch(device(p, i), g, p, sendb).start(), int(p == 3))
    mine = [pltpu.make_async_copy(smp.at[:, me * GB + g], recv.at[g, me], lsem.at[g]) for g in range(GB)]
    keep = pltpu.make_async_copy(bw.at[core], wfull.at[core], lsem.at[2])
    small = [
        pltpu.make_async_copy(sub_in, sub, lsem.at[3]),
        pltpu.make_async_copy(trn_in, trn, lsem.at[4]),
    ]
    for copy in mine + [keep] + small:
        copy.start()

    barrier = pltpu.get_barrier_semaphore()

    def greet(p, i):
        pl.semaphore_signal(barrier, inc=1, device_id=where(device(p, i)), device_id_type=MESH)

    for p in range(4):
        each(part, functools.partial(greet, p), int(p == 3))
    pl.semaphore_wait(barrier, n - 1)

    place = (plane + upper) % 2
    for g, p in groups:
        count = part - int(p == 3)
        ref = slots(sendb, g, p, count)
        pltpu.make_async_copy(ref, ref, fsem.at[g, p]).wait()
        tag = place if p < 2 else p
        each(part, lambda i: piece(device(p, i), g, tag).start(), int(p == 3))
    swap = pltpu.make_async_remote_copy(
        src_ref=bw.at[1 - core],
        dst_ref=wfull.at[core],
        send_sem=wsem.at[0],
        recv_sem=wsem.at[1],
        device_id={"sub": 1 - core},
        device_id_type=MESH,
    )
    swap.start()

    for copy in small:
        copy.wait()
    chosen = jnp.concatenate([sub[s : s + 1, :] for s in range(ns)], axis=1)
    picks = []
    for h in range(2):
        r = lax.broadcasted_iota(jnp.int32, (rows, chans), 0)
        if c_loc % 8 == 0:
            chan = r + h * rows
        else:
            chan = (h * half + r % half) * c_loc + r // half
        pick = jnp.where(chan == chosen, 1.0, 0.0).astype(F32)
        sel[h] = jnp.transpose(pick).astype(BF16)
        picks.append(pick.astype(BF16))
    keep.wait()
    swap.wait()
    sides = []
    for iq in range(2):
        cols = []
        for s in range(ns):
            cols.append(jnp.concatenate([jnp.transpose(wfull[h, s, iq]) for h in range(2)], axis=0))
        sides.append(jnp.concatenate(cols, axis=1))
    for s in range(ns):
        w_r, w_i = (jnp.concatenate([wfull[h, s, iq] for h in range(2)], axis=1) for iq in range(2))
        both = jnp.concatenate([w_r, w_i], axis=1)
        wv[s] = both
        hi, lo = split(jnp.concatenate([both, jnp.concatenate([-w_i, w_r], axis=1)], axis=0))
        bq[s, 0] = hi
        bq[s, 1] = lo
    w_hi, w_lo = split(jnp.concatenate(sides, axis=0))
    for h in range(2):
        wl[h, 0] = dot_t(w_hi, picks[h]).astype(BF16)
        wl[h, 1] = dot_t(w_lo, picks[h]).astype(BF16)

    def build(h, g):
        sides = []
        for iq in range(2):
            j = iq * c_loc
            if c_loc % 8 == 0:
                block = recv[g, pl.ds(h * half, half), j : j + c_loc, :].reshape(rows, pulses)
            else:
                block = jnp.concatenate(
                    [
                        recv[g, pl.ds(h * half, half), j + c : j + c + 1, :].reshape(half, pulses)
                        for c in range(c_loc)
                    ],
                    axis=0,
                )
            sides.append(block)
        return split(jnp.concatenate(sides, axis=1))

    def beam(h, z_hi, z_lo):
        l_hi, l_lo = wl[h, 0], wl[h, 1]
        return dot(l_hi, z_hi) + (dot(l_hi, z_lo) + dot(l_lo, z_hi))

    def report(d):
        return pltpu.make_async_remote_copy(
            src_ref=esend,
            dst_ref=erecv.at[me],
            send_sem=esem.at[0],
            recv_sem=esem.at[1],
            device_id=where(d),
            device_id_type=MESH,
        )

    def wait_for(g, p):
        if p == 3:
            mine[g].wait()
        ref = slots(recv, g, p, part - int(p == 3))
        arrived(ref, ref, p, g).wait_recv()

    factor = 1.0 / (GB * pulses)
    for g in range(GB):
        wait_for(g, 3)
        wait_for(g, 2)
        z_hi, z_lo = build(upper, g)
        eacc[...] = beam(upper, z_hi, z_lo)
        picked = sel[upper]
        gat[0] = dot(picked, z_hi).astype(BF16)
        gat[1] = dot(picked, z_lo).astype(BF16)
        wait_for(g, 0)
        wait_for(g, 1)
        z_hi, z_lo = build(1 - upper, g)
        full = eacc[...] + beam(1 - upper, z_hi, z_lo)
        e_re = full[:beams, :pulses] + full[beams:, pulses:]
        e_im = full[:beams, pulses:] - full[beams:, :pulses]
        power = e_re * e_re + e_im * e_im
        ev[g, 0] = e_re
        ev[g, 1] = e_im
        if g < GB - 1:
            psum[...] = power if g == 0 else psum[...] + power
        else:
            p_hi, p_lo = split(psum[...] + power)
            ones = jnp.ones((8, pulses), BF16)
            esum = (dot_t(ones, p_hi) + dot_t(ones, p_lo))[0:1]
            esend[...] = esum
            erecv[me] = esum
            for j in range(3):
                other = j + (j + 4 - plane) // 4
                each(part, lambda i: report(other * part + (low + i) % part).start())
            each(part, lambda i: report(device(3, i)).start(), 1)
        picked = sel[1 - upper]
        gat[0] = (gat[0].astype(F32) + dot(picked, z_hi)).astype(BF16)
        gat[1] = (gat[1].astype(F32) + dot(picked, z_lo)).astype(BF16)
        weight = trn[g].astype(F32) * factor
        total = jnp.zeros((s_n, 2 * beams), F32)
        for s in range(ns):
            x = [gat[i, s * s_n : (s + 1) * s_n, :] for i in range(2)]
            right = [
                jnp.concatenate([v, jnp.concatenate([-v[:, pulses:], v[:, :pulses]], axis=1)], axis=0)
                for v in x
            ]
            r_s = (dot_t(x[0], right[0]) + (dot_t(x[0], right[1]) + dot_t(x[1], right[0]))) * weight
            if g > 0:
                r_s = cov[s] + r_s
            cov[s] = r_s
            if g == GB - 1:
                r_hi, r_lo = split(r_s)
                b_hi, b_lo = bq[s, 0], bq[s, 1]
                total = total + (dot(r_hi, b_hi) + (dot(r_lo, b_hi) + dot(r_hi, b_lo))) * wv[s]
    quadratic = jnp.sum(total, axis=0, keepdims=True)
    quadratic = quadratic[:, :beams] + quadratic[:, beams:]
    inverse = 1.0 / jnp.sqrt(quadratic + loading)
    scale = jnp.transpose(jnp.broadcast_to(inverse, (pulses, beams)))
    for g in range(GB):
        for iq in range(2):
            filt[iq, pl.ds(g, beams, stride=GB), :] = ev[g, iq] * scale

    sent = sendb.at[:, pl.ds(0, n - 1)]
    pltpu.make_async_remote_copy(
        src_ref=sent,
        dst_ref=sent,
        send_sem=send_sem.at[0],
        recv_sem=recv_sem.at[0, 0],
        device_id=where(device(2, 0)),
        device_id_type=MESH,
    ).wait_send()
    reports = erecv.at[pl.ds(0, n - 1)]
    shared = pltpu.make_async_remote_copy(
        src_ref=reports,
        dst_ref=reports,
        send_sem=esem.at[0],
        recv_sem=esem.at[1],
        device_id=where(device(2, 0)),
        device_id_type=MESH,
    )
    shared.wait_send()
    shared.wait_recv()
    en[...] = jnp.sum(erecv[...], axis=0) * (1.0 / (gates * pulses))


def store(cov, filt, en, cov_out, filt_out, en_out, sem):
    pairs = ((cov, cov_out), (filt, filt_out), (en, en_out))
    copies = [pltpu.make_async_copy(a, b, sem.at[i]) for i, (a, b) in enumerate(pairs)]
    for copy in copies:
        copy.start()
    for copy in copies:
        copy.wait()


def body(samples, beam_weights, subarrays, training):
    range_count = lax.axis_size("range")
    cores = lax.axis_size("sub")
    n = range_count * cores
    parts_iq, c_loc, gates, pulses = samples.shape
    blocks, ns, _, s_n, k_half = beam_weights.shape
    assert gates == GB * n and blocks == cores == 2 and subarrays.shape[0] == 1
    assert n & (n - 1) == 0 and n >= 8
    assert parts_iq == 2 and n * c_loc == ns * s_n
    beams, chans = 2 * k_half, n * c_loc
    dims = (n, cores, c_loc, gates, pulses, ns, s_n, k_half)
    hbm = pl.BlockSpec(memory_space=pl.ANY)
    vmem = pl.BlockSpec(memory_space=pltpu.VMEM)
    dma = pltpu.SemaphoreType.DMA
    cov, filt, en = pl.pallas_call(
        functools.partial(kernel, dims),
        out_shape=(
            pltpu.VMEM((ns, s_n, 2 * s_n), F32),
            pltpu.VMEM((2, beams * GB, pulses), F32),
            pltpu.VMEM((1, beams), F32),
        ),
        in_specs=[hbm] * 4,
        out_specs=(vmem, vmem, vmem),
        scratch_shapes=[
            pltpu.VMEM((ns, s_n), jnp.int32),
            pltpu.SMEM((GB,), jnp.int32),
            pltpu.VMEM((GB, n, 2 * c_loc, pulses), F32),
            pltpu.VMEM((GB, n, 2 * c_loc, pulses), F32),
            pltpu.VMEM((2, ns, 2, s_n, k_half), F32),
            pltpu.VMEM((2, chans, chans // 2), BF16),
            pltpu.VMEM((2, 2, 2 * beams, chans // 2), BF16),
            pltpu.VMEM((ns, 2, 2 * s_n, 2 * beams), BF16),
            pltpu.VMEM((ns, s_n, 2 * beams), F32),
            pltpu.VMEM((2 * beams, 2 * pulses), F32),
            pltpu.VMEM((2, chans, 2 * pulses), BF16),
            pltpu.VMEM((GB, 2, beams, pulses), F32),
            pltpu.VMEM((beams, pulses), F32),
            pltpu.VMEM((1, beams), F32),
            pltpu.VMEM((n, 1, beams), F32),
            dma((1,)),
            dma((GB, 4)),
            dma((GB, 4)),
            dma((2,)),
            dma((2,)),
            dma((5,)),
        ],
        compiler_params=pltpu.CompilerParams(collective_id=0, has_side_effects=True),
    )(
        samples.reshape(2 * c_loc, gates, pulses),
        beam_weights,
        subarrays.reshape(ns, s_n),
        training,
    )
    cov, filt, en = (pltpu.with_memory_space_constraint(v, pltpu.VMEM) for v in (cov, filt, en))
    cov, filt, en = pl.pallas_call(
        store,
        out_shape=[jax.ShapeDtypeStruct(v.shape, F32) for v in (cov, filt, en)],
        in_specs=[vmem] * 3,
        out_specs=[hbm] * 3,
        scratch_shapes=[dma((3,))],
    )(cov, filt, en)
    return (
        cov.reshape(1, ns, s_n, 2 * s_n),
        filt.reshape(2, beams, GB, pulses),
        en.reshape(beams),
    )


def solution(mesh):
    placed = (
        P(None, ("groups", "range", "sub"), None, None),
        P(("groups", "range"), None, None, None, "sub"),
        P(("groups", "range", "sub"), None, None),
        P(("groups", "range", "sub")),
    )
    return jax.shard_map(
        body,
        mesh=mesh,
        in_specs=placed,
        out_specs=(
            P(("groups", "range", "sub"), None, None, None),
            P(None, None, ("groups", "range", "sub"), None),
            P("groups"),
        ),
        check_vma=False,
    )
```

time: 36.8 us -> 36.3 us (0.986)
  Pallas kernels: 36 us -> 35.5 us
    pallas_call x1, Pallas kernels: 35.2 us -> 34.7 us  [body(): pl.pallas_call(functools.partial(kernel, dims), out_shape=(pltpu.VMEM((ns...]
where the time goes in v1:
time: 36.3 us; the launch traced here: 36.1 us
  Pallas kernels  35.5 us (98%)
  between operations  0.64 us (2%)
    pallas_call x1, Pallas kernels, body(): pl.pallas_call(functools.partial(kernel, dims), out_shape=(pltpu.VMEM((ns...  34.7 us
    pallas_call x1, Pallas kernels, body(): pl.pallas_call(store, out_shape=[jax.ShapeDtypeStruct(v.shape, F32) for v...  0.82 us

profile of v1, /device:TPU:0, one launch (start us, length us, event | category | flops | bytes accessed | tf_op | source)
XLA Modules:
  0.0 36.1 jit_solution(12124340314844131160)
XLA Ops:
  0.6 34.7 %shard_map.67 = (f32[8,64,128]{2,1,0:T(8,128)S(1)}, f32[2,256,128]{2,1,0:T(8,128)S(1)}, f32[1,128]{1,0:T(1,128)S(1)}) custom-call(f32[64,32,128]{2,1,0:T(8,128)} %bitcast.5, f32[2,8,2,64,64]{4,3,2,1,0:T(8,128)} %bw.1, s32[8,64]{1,0:T(8,128)} %bitcast.6, s32[2]{0:T(128)} %trn_in.1), custom_call_target="tpu_custom_call" | custom-call | tf_op jit(solution)/shard_map/pallas_call | solution.py:304
  35.3 0.8 %shard_map.68 = (f32[8,64,128]{2,1,0:T(8,128)}, f32[2,256,128]{2,1,0:T(8,128)}, f32[1,128]{1,0:T(1,128)}) custom-call(f32[8,64,128]{2,1,0:T(8,128)S(1)} %get-tuple-element.9.cov, f32[2,256,128]{2,1,0:T(8,128)S(1)} %get-tuple-element.10.filt, f32[1,128]{1,0:T(1,128)S(1)} %get-tuple-element.11.en), custom_call_target="tpu_custom_call" | custom-call | tf_op jit(solution)/shard_map/pallas_call | solution.py:344

commit v2 on v1

--- a/solution.py
+++ b/solution.py
@@ -45,7 +45,7 @@
     smp, bw, sub_in, trn_in,
     cov, filt, en,
     sub, trn, sendb, recv, wfull, sel, wl, bq, wv, eacc, gat, ev, psum, esend, erecv,
-    send_sem, recv_sem, fsem, wsem, esem, lsem,
+    send_sem, recv_sem, fsem, wsem, esem, lsem, near,
 ):
     n, cores, c_loc, gates, pulses, ns, s_n, k_half = dims
     beams = 2 * k_half
@@ -103,21 +103,90 @@
         copy.start()
 
     barrier = pltpu.get_barrier_semaphore()
-
-    def greet(p, i):
-        pl.semaphore_signal(barrier, inc=1, device_id=where(device(p, i)), device_id_type=MESH)
-
-    for p in range(4):
-        each(part, functools.partial(greet, p), int(p == 3))
-    pl.semaphore_wait(barrier, n - 1)
-
+    below, above = (plane + 3) // 4, (6 - plane) // 4
+    inner = below * above == 1
     place = (plane + upper) % 2
-    for g, p in groups:
-        count = part - int(p == 3)
-        ref = slots(sendb, g, p, count)
+    cell = low - core
+
+    def greet(d):
+        pl.semaphore_signal(barrier, inc=1, device_id=where(d), device_id_type=MESH)
+
+    def tell(k):
+        for there, step in ((above, part), (below, -part)):
+
+            @pl.when(there == 1)
+            def _():
+                pl.semaphore_signal(
+                    near.at[k], inc=1, device_id=where(me + step), device_id_type=MESH
+                )
+
+    for there, step in ((below, -part), (above, part)):
+
+        @pl.when(there == 1)
+        def _():
+            for j in range(cores):
+                greet(me - core + step + j)
+
+    each(part, lambda i: greet(device(3, i)), 1)
+
+    def send(p, i, g):
+        piece(device(p, i), g, place if p < 2 else p).start()
+
+    def send_plane(p, g):
+        each(part, lambda i: send(p, i, g), int(p == 3))
+
+    def facing(j, g):
+        piece(planes[1] * part + cell + j, g, place).start()
+
+    def others(g):
+        each(part - cores, lambda i: piece(planes[1] * part + (cell + cores + i) % part, g, place).start())
+
+    for g, p in groups[: 2 * GB]:
+        ref = slots(sendb, g, p)
         pltpu.make_async_copy(ref, ref, fsem.at[g, p]).wait()
-        tag = place if p < 2 else p
-        each(part, lambda i: piece(device(p, i), g, tag).start(), int(p == 3))
+    pl.semaphore_wait(barrier, part - 1 + cores * (below + above))
+    tell(0)
+
+    @pl.when(inner)
+    def _():
+        for g in range(GB):
+            for j in range(cores):
+                facing(j, g)
+
+    pl.semaphore_wait(near.at[0], below + above)
+    tell(1)
+
+    @pl.when(inner)
+    def _():
+        for g in range(GB - 1):
+            others(g)
+
+    pl.semaphore_wait(near.at[1], below + above)
+    tell(2)
+
+    @pl.when(inner)
+    def _():
+        for g in range(GB):
+            send_plane(0, g)
+        others(GB - 1)
+
+    @pl.when(jnp.logical_not(inner))
+    def _():
+        send_plane(1, 0)
+
+    pl.semaphore_wait(near.at[2], below + above)
+
+    @pl.when(jnp.logical_not(inner))
+    def _():
+        for g in range(GB):
+            send_plane(0, g)
+        for g in range(1, GB):
+            send_plane(1, g)
+
+    for g, p in groups[2 * GB :]:
+        ref = slots(sendb, g, p, part - int(p == 3))
+        pltpu.make_async_copy(ref, ref, fsem.at[g, p]).wait()
+        send_plane(p, g)
     swap = pltpu.make_async_remote_copy(
         src_ref=bw.at[1 - core],
         dst_ref=wfull.at[core],
@@ -332,6 +401,7 @@
             dma((2,)),
             dma((2,)),
             dma((5,)),
+            pltpu.SemaphoreType.REGULAR((3,)),
         ],
         compiler_params=pltpu.CompilerParams(collective_id=0, has_side_effects=True),
     )(

time: 36.3 us -> 34.3 us (0.945)
  Pallas kernels: 35.5 us -> 33.5 us
    pallas_call x1, Pallas kernels: 34.7 us -> 32.7 us  [body(): pl.pallas_call(functools.partial(kernel, dims), out_shape=(pltpu.VMEM((ns...]
where the time goes in v2:
time: 34.3 us; the launch traced here: 34.2 us
  Pallas kernels  33.5 us (98%)
  between operations  0.64 us (2%)
    pallas_call x1, Pallas kernels, body(): pl.pallas_call(functools.partial(kernel, dims), out_shape=(pltpu.VMEM((ns...  32.7 us
    pallas_call x1, Pallas kernels, body(): pl.pallas_call(store, out_shape=[jax.ShapeDtypeStruct(v.shape, F32) for v...  0.82 us

profile of v2, /device:TPU:0, one launch (start us, length us, event | category | flops | bytes accessed | tf_op | source)
XLA Modules:
  0.0 34.2 jit_solution(984767051676054911)
XLA Ops:
  0.6 32.7 %shard_map.67 = (f32[8,64,128]{2,1,0:T(8,128)S(1)}, f32[2,256,128]{2,1,0:T(8,128)S(1)}, f32[1,128]{1,0:T(1,128)S(1)}) custom-call(f32[64,32,128]{2,1,0:T(8,128)} %bitcast.5, f32[2,8,2,64,64]{4,3,2,1,0:T(8,128)} %bw.1, s32[8,64]{1,0:T(8,128)} %bitcast.6, s32[2]{0:T(128)} %trn_in.1), custom_call_target="tpu_custom_call" | custom-call | tf_op jit(solution)/shard_map/pallas_call | solution.py:373
  33.4 0.8 %shard_map.68 = (f32[8,64,128]{2,1,0:T(8,128)}, f32[2,256,128]{2,1,0:T(8,128)}, f32[1,128]{1,0:T(1,128)}) custom-call(f32[8,64,128]{2,1,0:T(8,128)S(1)} %get-tuple-element.9.cov, f32[2,256,128]{2,1,0:T(8,128)S(1)} %get-tuple-element.10.filt, f32[1,128]{1,0:T(1,128)S(1)} %get-tuple-element.11.en), custom_call_target="tpu_custom_call" | custom-call | tf_op jit(solution)/shard_map/pallas_call | solution.py:414

commit v3 on v1

--- a/solution.py
+++ b/solution.py
@@ -45,13 +45,13 @@
     smp, bw, sub_in, trn_in,
     cov, filt, en,
     sub, trn, sendb, recv, wfull, sel, wl, bq, wv, eacc, gat, ev, psum, esend, erecv,
-    send_sem, recv_sem, fsem, wsem, esem, lsem,
+    send_sem, recv_sem, fsem, wsem, esem, lsem, near,
 ):
     n, cores, c_loc, gates, pulses, ns, s_n, k_half = dims
     beams = 2 * k_half
     chans = n * c_loc
-    part, half = n // 4, n // 2
-    rows = half * c_loc
+    part = n // 4
+    rows = part * c_loc
     core = lax.axis_index("sub")
     me = lax.axis_index("range") * cores + core
     plane, low = me // part, me % part
@@ -90,7 +90,22 @@
             device_id_type=MESH,
         )
 
-    groups = [(g, p) for g in range(GB) for p in (0, 1)] + [(g, p) for g in range(GB) for p in (2, 3)]
+    barrier = pltpu.get_barrier_semaphore()
+    below, above = (plane + 3) // 4, (6 - plane) // 4
+
+    def greet(d):
+        pl.semaphore_signal(barrier, inc=1, device_id=where(d), device_id_type=MESH)
+
+    for there, step in ((below * above, -part), (above, part)):
+
+        @pl.when(there == 1)
+        def _():
+            for j in range(cores):
+                greet(me - core + step + j)
+
+    each(part, lambda i: greet(device(3, i)), 1)
+
+    groups = [(g, p) for p in (1, 0, 2, 3) for g in range(GB)]
     for g, p in groups:
         each(part, lambda i: fetch(device(p, i), g, p, sendb).start(), int(p == 3))
     mine = [pltpu.make_async_copy(smp.at[:, me * GB + g], recv.at[g, me], lsem.at[g]) for g in range(GB)]
@@ -102,22 +117,103 @@
     for copy in mine + [keep] + small:
         copy.start()
 
-    barrier = pltpu.get_barrier_semaphore()
-
-    def greet(p, i):
-        pl.semaphore_signal(barrier, inc=1, device_id=where(device(p, i)), device_id_type=MESH)
-
-    for p in range(4):
-        each(part, functools.partial(greet, p), int(p == 3))
-    pl.semaphore_wait(barrier, n - 1)
+    def ready(g, p):
+        ref = slots(sendb, g, p, part - int(p == 3))
+        pltpu.make_async_copy(ref, ref, fsem.at[g, p]).wait()
 
     place = (plane + upper) % 2
-    for g, p in groups:
-        count = part - int(p == 3)
-        ref = slots(sendb, g, p, count)
-        pltpu.make_async_copy(ref, ref, fsem.at[g, p]).wait()
-        tag = place if p < 2 else p
-        each(part, lambda i: piece(device(p, i), g, tag).start(), int(p == 3))
+    cell = low - core
+
+    def send(p, i, g):
+        piece(device(p, i), g, place if p < 2 else p).start()
+
+    def send_plane(p, g):
+        each(part, lambda i: send(p, i, g), int(p == 3))
+
+    def facing(j, g):
+        piece(planes[1] * part + cell + j, g, place).start()
+
+    def others(g):
+        each(part - cores, lambda i: piece(planes[1] * part + (cell + cores + i) % part, g, place).start())
+
+    def tell(step, k):
+        pl.semaphore_signal(near.at[k], inc=1, device_id=where(me + step), device_id_type=MESH)
+
+    def hear(k):
+        pl.semaphore_wait(near.at[k], 1)
+
+    ready(0, 1)
+    pl.semaphore_wait(barrier, part - 1 + cores * (below + above * (1 - upper)))
+
+    @pl.when(plane == 0)
+    def _():
+        tell(part, 2)
+        for g, p in groups[1 : 2 * GB]:
+            ready(g, p)
+        hear(0)
+        for j in range(cores):
+            facing(j, 0)
+        hear(1)
+        others(0)
+        hear(2)
+        send_plane(0, 0)
+        send_plane(0, 1)
+        for j in range(cores):
+            each(part // cores, lambda i: piece(planes[1] * part + (cell + cores * i) % part + j, 1, place).start())
+
+    @pl.when(plane == 1)
+    def _():
+        tell(part, 0)
+        tell(-part, 0)
+        for j in range(cores):
+            facing(j, 0)
+        for g, p in groups[1 : 2 * GB]:
+            ready(g, p)
+        hear(0)
+        tell(-part, 1)
+        others(0)
+        hear(2)
+        tell(part, 1)
+        hear(1)
+        tell(-part, 2)
+        send_plane(0, 0)
+        send_plane(0, 1)
+        for j in range(cores):
+            each(part // cores, lambda i: piece(planes[1] * part + (cell + cores * i) % part + j, 1, place).start())
+
+    @pl.when(plane == 2)
+    def _():
+        tell(-part, 0)
+        for j in range(cores):
+            facing(j, 0)
+        for g, p in groups[1 : 2 * GB]:
+            ready(g, p)
+        hear(0)
+        others(0)
+        hear(2)
+        tell(-part, 1)
+        hear(1)
+        tell(part, 0)
+        send_plane(0, 0)
+        send_plane(0, 1)
+        for j in range(cores):
+            each(part // cores, lambda i: piece(planes[1] * part + (cell + cores * i) % part + j, 1, place).start())
+
+    @pl.when(plane == 3)
+    def _():
+        tell(-part, 2)
+        for g, p in groups[1 : 2 * GB]:
+            ready(g, p)
+        hear(0)
+        send_plane(1, 0)
+        send_plane(0, 0)
+        send_plane(0, 1)
+        for j in range(cores):
+            each(part // cores, lambda i: piece(planes[1] * part + (cell + cores * i) % part + j, 1, place).start())
+
+    for g, p in groups[2 * GB :]:
+        ready(g, p)
+        send_plane(p, g)
     swap = pltpu.make_async_remote_copy(
         src_ref=bw.at[1 - core],
         dst_ref=wfull.at[core],
@@ -132,14 +228,14 @@
         copy.wait()
     chosen = jnp.concatenate([sub[s : s + 1, :] for s in range(ns)], axis=1)
     picks = []
-    for h in range(2):
+    for q in range(4):
         r = lax.broadcasted_iota(jnp.int32, (rows, chans), 0)
         if c_loc % 8 == 0:
-            chan = r + h * rows
+            chan = r + q * rows
         else:
-            chan = (h * half + r % half) * c_loc + r // half
+            chan = (q * part + r % part) * c_loc + r // part
         pick = jnp.where(chan == chosen, 1.0, 0.0).astype(F32)
-        sel[h] = jnp.transpose(pick).astype(BF16)
+        sel[q] = jnp.transpose(pick).astype(BF16)
         picks.append(pick.astype(BF16))
     keep.wait()
     swap.wait()
@@ -157,20 +253,21 @@
         bq[s, 0] = hi
         bq[s, 1] = lo
     w_hi, w_lo = split(jnp.concatenate(sides, axis=0))
-    for h in range(2):
-        wl[h, 0] = dot_t(w_hi, picks[h]).astype(BF16)
-        wl[h, 1] = dot_t(w_lo, picks[h]).astype(BF16)
-
-    def build(h, g):
+    for q in range(4):
+        wl[q, 0] = dot_t(w_hi, picks[q]).astype(BF16)
+        wl[q, 1] = dot_t(w_lo, picks[q]).astype(BF16)
+
+    def build(p, g):
+        q = planes[p]
         sides = []
         for iq in range(2):
             j = iq * c_loc
             if c_loc % 8 == 0:
-                block = recv[g, pl.ds(h * half, half), j : j + c_loc, :].reshape(rows, pulses)
+                block = recv[g, pl.ds(q * part, part), j : j + c_loc, :].reshape(rows, pulses)
             else:
                 block = jnp.concatenate(
                     [
-                        recv[g, pl.ds(h * half, half), j + c : j + c + 1, :].reshape(half, pulses)
+                        recv[g, pl.ds(q * part, part), j + c : j + c + 1, :].reshape(part, pulses)
                         for c in range(c_loc)
                     ],
                     axis=0,
@@ -178,9 +275,15 @@
             sides.append(block)
         return split(jnp.concatenate(sides, axis=1))
 
-    def beam(h, z_hi, z_lo):
-        l_hi, l_lo = wl[h, 0], wl[h, 1]
-        return dot(l_hi, z_hi) + (dot(l_hi, z_lo) + dot(l_lo, z_hi))
+    def beam(p, z_hi, z_lo):
+        l_hi, l_lo = wl[planes[p], 0], wl[planes[p], 1]
+        both = dot(jnp.concatenate([l_hi, l_lo], axis=1), jnp.concatenate([z_hi, z_hi], axis=0))
+        return both + dot(l_hi, z_lo)
+
+    def gather(p, z):
+        picked = sel[planes[p]]
+        for i in range(2):
+            gat[i] = (gat[i].astype(F32) + dot(picked, z[i])).astype(BF16)
 
     def report(d):
         return pltpu.make_async_remote_copy(
@@ -202,37 +305,36 @@
     for g in range(GB):
         wait_for(g, 3)
         wait_for(g, 2)
-        z_hi, z_lo = build(upper, g)
-        eacc[...] = beam(upper, z_hi, z_lo)
-        picked = sel[upper]
-        gat[0] = dot(picked, z_hi).astype(BF16)
-        gat[1] = dot(picked, z_lo).astype(BF16)
+        own, next_to = build(3, g), build(2, g)
+        eacc[...] = beam(3, *own) + beam(2, *next_to)
+        picked = jnp.concatenate([sel[planes[3]], sel[planes[2]]], axis=1)
+        for i in range(2):
+            gat[i] = dot(picked, jnp.concatenate([own[i], next_to[i]], axis=0)).astype(BF16)
         wait_for(g, 0)
+        z = build(0, g)
+        eacc[...] = eacc[...] + beam(0, *z)
+        gather(0, z)
         wait_for(g, 1)
-        z_hi, z_lo = build(1 - upper, g)
-        full = eacc[...] + beam(1 - upper, z_hi, z_lo)
+        z = build(1, g)
+        full = eacc[...] + beam(1, *z)
         e_re = full[:beams, :pulses] + full[beams:, pulses:]
         e_im = full[:beams, pulses:] - full[beams:, :pulses]
         power = e_re * e_re + e_im * e_im
-        ev[g, 0] = e_re
-        ev[g, 1] = e_im
         if g < GB - 1:
             psum[...] = power if g == 0 else psum[...] + power
         else:
-            p_hi, p_lo = split(psum[...] + power)
-            ones = jnp.ones((8, pulses), BF16)
-            esum = (dot_t(ones, p_hi) + dot_t(ones, p_lo))[0:1]
+            across = jnp.transpose(psum[...] + power)
+            esum = jnp.sum(across.reshape(pulses // 8, 8, beams), axis=0)
             esend[...] = esum
             erecv[me] = esum
             for j in range(3):
                 other = j + (j + 4 - plane) // 4
                 each(part, lambda i: report(other * part + (low + i) % part).start())
             each(part, lambda i: report(device(3, i)).start(), 1)
-        picked = sel[1 - upper]
-        gat[0] = (gat[0].astype(F32) + dot(picked, z_hi)).astype(BF16)
-        gat[1] = (gat[1].astype(F32) + dot(picked, z_lo)).astype(BF16)
+        ev[g, 0] = e_re
+        ev[g, 1] = e_im
+        gather(1, z)
         weight = trn[g].astype(F32) * factor
-        total = jnp.zeros((s_n, 2 * beams), F32)
         for s in range(ns):
             x = [gat[i, s * s_n : (s + 1) * s_n, :] for i in range(2)]
             right = [
@@ -240,13 +342,13 @@
                 for v in x
             ]
             r_s = (dot_t(x[0], right[0]) + (dot_t(x[0], right[1]) + dot_t(x[1], right[0]))) * weight
-            if g > 0:
-                r_s = cov[s] + r_s
-            cov[s] = r_s
-            if g == GB - 1:
-                r_hi, r_lo = split(r_s)
-                b_hi, b_lo = bq[s, 0], bq[s, 1]
-                total = total + (dot(r_hi, b_hi) + (dot(r_lo, b_hi) + dot(r_hi, b_lo))) * wv[s]
+            cov[s] = r_s if g == 0 else cov[s] + r_s
+    total = jnp.zeros((8, 2 * beams), F32)
+    for s in range(ns):
+        r_hi, r_lo = split(cov[s])
+        b_hi, b_lo = bq[s, 0], bq[s, 1]
+        term = (dot(r_hi, b_hi) + (dot(r_lo, b_hi) + dot(r_hi, b_lo))) * wv[s]
+        total = total + jnp.sum(term.reshape(s_n // 8, 8, 2 * beams), axis=0)
     quadratic = jnp.sum(total, axis=0, keepdims=True)
     quadratic = quadratic[:, :beams] + quadratic[:, beams:]
     inverse = 1.0 / jnp.sqrt(quadratic + loading)
@@ -275,7 +377,7 @@
     )
     shared.wait_send()
     shared.wait_recv()
-    en[...] = jnp.sum(erecv[...], axis=0) * (1.0 / (gates * pulses))
+    en[...] = jnp.sum(jnp.sum(erecv[...], axis=0), axis=0, keepdims=True) * (1.0 / (gates * pulses))
 
 
 def store(cov, filt, en, cov_out, filt_out, en_out, sem):
@@ -316,22 +418,23 @@
             pltpu.VMEM((GB, n, 2 * c_loc, pulses), F32),
             pltpu.VMEM((GB, n, 2 * c_loc, pulses), F32),
             pltpu.VMEM((2, ns, 2, s_n, k_half), F32),
-            pltpu.VMEM((2, chans, chans // 2), BF16),
-            pltpu.VMEM((2, 2, 2 * beams, chans // 2), BF16),
+            pltpu.VMEM((4, chans, chans // 4), BF16),
+            pltpu.VMEM((4, 2, 2 * beams, chans // 4), BF16),
             pltpu.VMEM((ns, 2, 2 * s_n, 2 * beams), BF16),
             pltpu.VMEM((ns, s_n, 2 * beams), F32),
             pltpu.VMEM((2 * beams, 2 * pulses), F32),
             pltpu.VMEM((2, chans, 2 * pulses), BF16),
             pltpu.VMEM((GB, 2, beams, pulses), F32),
             pltpu.VMEM((beams, pulses), F32),
-            pltpu.VMEM((1, beams), F32),
-            pltpu.VMEM((n, 1, beams), F32),
+            pltpu.VMEM((8, beams), F32),
+            pltpu.VMEM((n, 8, beams), F32),
             dma((1,)),
             dma((GB, 4)),
             dma((GB, 4)),
             dma((2,)),
             dma((2,)),
             dma((5,)),
+            pltpu.SemaphoreType.REGULAR((3,)),
         ],
         compiler_params=pltpu.CompilerParams(collective_id=0, has_side_effects=True),
     )(

time: 36.3 us -> 33.9 us (0.934)
  Pallas kernels: 35.5 us -> 33.1 us
    pallas_call x1, Pallas kernels: 34.7 us -> 32.2 us  [body(): pl.pallas_call(functools.partial(kernel, dims), out_shape=(pltpu.VMEM((ns...]
where the time goes in v3:
time: 33.9 us; the launch traced here: 33.7 us
  Pallas kernels  33.1 us (98%)
  between operations  0.64 us (2%)
    pallas_call x1, Pallas kernels, body(): pl.pallas_call(functools.partial(kernel, dims), out_shape=(pltpu.VMEM((ns...  32.2 us
    pallas_call x1, Pallas kernels, body(): pl.pallas_call(store, out_shape=[jax.ShapeDtypeStruct(v.shape, F32) for v...  0.82 us

profile of v3, /device:TPU:0, one launch (start us, length us, event | category | flops | bytes accessed | tf_op | source)
XLA Modules:
  0.0 33.7 jit_solution(15812527292524747893)
XLA Ops:
  0.6 32.2 %shard_map.67 = (f32[8,64,128]{2,1,0:T(8,128)S(1)}, f32[2,256,128]{2,1,0:T(8,128)S(1)}, f32[1,128]{1,0:T(1,128)S(1)}) custom-call(f32[64,32,128]{2,1,0:T(8,128)} %bitcast.5, f32[2,8,2,64,64]{4,3,2,1,0:T(8,128)} %bw.1, s32[8,64]{1,0:T(8,128)} %bitcast.6, s32[2]{0:T(128)} %trn_in.1), custom_call_target="tpu_custom_call" | custom-call | tf_op jit(solution)/shard_map/pallas_call | solution.py:406
  32.9 0.8 %shard_map.68 = (f32[8,64,128]{2,1,0:T(8,128)}, f32[2,256,128]{2,1,0:T(8,128)}, f32[1,128]{1,0:T(1,128)}) custom-call(f32[8,64,128]{2,1,0:T(8,128)S(1)} %get-tuple-element.9.cov, f32[2,256,128]{2,1,0:T(8,128)S(1)} %get-tuple-element.10.filt, f32[1,128]{1,0:T(1,128)S(1)} %get-tuple-element.11.en), custom_call_target="tpu_custom_call" | custom-call | tf_op jit(solution)/shard_map/pallas_call | solution.py:447

commit v4 on v3

--- a/solution.py
+++ b/solution.py
@@ -45,7 +45,7 @@
     smp, bw, sub_in, trn_in,
     cov, filt, en,
     sub, trn, sendb, recv, wfull, sel, wl, bq, wv, eacc, gat, ev, psum, esend, erecv,
-    send_sem, recv_sem, fsem, wsem, esem, lsem, near,
+    send_sem, recv_sem, fsem, rsem, lsem, near,
 ):
     n, cores, c_loc, gates, pulses, ns, s_n, k_half = dims
     beams = 2 * k_half
@@ -68,14 +68,14 @@
         return ref.at[g, pl.ds(planes[p] * part, count or part)]
 
     def fetch(d, g, p, ref):
-        return pltpu.make_async_copy(smp.at[:, d * GB + g], ref.at[g, d], fsem.at[g, p])
+        return pltpu.make_async_copy(smp.at[:, d * GB + g], ref.at[g, d], fsem.at[GB + min(p, 2) // 2 if p != 1 else g])
 
     def piece(d, g, p):
         return pltpu.make_async_remote_copy(
             src_ref=sendb.at[g, d],
             dst_ref=recv.at[g, me],
             send_sem=send_sem.at[0],
-            recv_sem=recv_sem.at[g, p],
+            recv_sem=recv_sem.at[g, min(p, 2) if isinstance(p, int) else p],
             device_id=where(d),
             device_id_type=MESH,
         )
@@ -108,18 +108,21 @@
     groups = [(g, p) for p in (1, 0, 2, 3) for g in range(GB)]
     for g, p in groups:
         each(part, lambda i: fetch(device(p, i), g, p, sendb).start(), int(p == 3))
-    mine = [pltpu.make_async_copy(smp.at[:, me * GB + g], recv.at[g, me], lsem.at[g]) for g in range(GB)]
-    keep = pltpu.make_async_copy(bw.at[core], wfull.at[core], lsem.at[2])
+    mine = [pltpu.make_async_copy(smp.at[:, me * GB + g], recv.at[g, me], lsem.at[0]) for g in range(GB)]
+    keep = pltpu.make_async_copy(bw.at[core], wfull.at[core], lsem.at[1])
     small = [
-        pltpu.make_async_copy(sub_in, sub, lsem.at[3]),
-        pltpu.make_async_copy(trn_in, trn, lsem.at[4]),
+        pltpu.make_async_copy(sub_in, sub, lsem.at[2]),
+        pltpu.make_async_copy(trn_in, trn, lsem.at[3]),
     ]
     for copy in mine + [keep] + small:
         copy.start()
 
-    def ready(g, p):
-        ref = slots(sendb, g, p, part - int(p == 3))
-        pltpu.make_async_copy(ref, ref, fsem.at[g, p]).wait()
+    def ready(k):
+        ref = (
+            [slots(sendb, g, 1) for g in range(GB)]
+            + [sendb.at[:, pl.ds(0, part)], sendb.at[:, pl.ds(0, 2 * part - 1)]]
+        )[k]
+        pltpu.make_async_copy(ref, ref, fsem.at[k]).wait()
 
     place = (plane + upper) % 2
     cell = low - core
@@ -142,14 +145,14 @@
     def hear(k):
         pl.semaphore_wait(near.at[k], 1)
 
-    ready(0, 1)
+    ready(0)
     pl.semaphore_wait(barrier, part - 1 + cores * (below + above * (1 - upper)))
 
     @pl.when(plane == 0)
     def _():
         tell(part, 2)
-        for g, p in groups[1 : 2 * GB]:
-            ready(g, p)
+        for k in range(1, GB + 1):
+            ready(k)
         hear(0)
         for j in range(cores):
             facing(j, 0)
@@ -158,8 +161,9 @@
         hear(2)
         send_plane(0, 0)
         send_plane(0, 1)
-        for j in range(cores):
-            each(part // cores, lambda i: piece(planes[1] * part + (cell + cores * i) % part + j, 1, place).start())
+        each(part // cores, lambda i: piece(planes[1] * part + part - cores * (i + 1), 1, place).start())
+        for j in range(1, cores):
+            each(part // cores, lambda i: piece(planes[1] * part + (cell + cores * (i + 1)) % part + j, 1, place).start())
 
     @pl.when(plane == 1)
     def _():
@@ -167,8 +171,8 @@
         tell(-part, 0)
         for j in range(cores):
             facing(j, 0)
-        for g, p in groups[1 : 2 * GB]:
-            ready(g, p)
+        for k in range(1, GB + 1):
+            ready(k)
         hear(0)
         tell(-part, 1)
         others(0)
@@ -178,16 +182,17 @@
         tell(-part, 2)
         send_plane(0, 0)
         send_plane(0, 1)
-        for j in range(cores):
-            each(part // cores, lambda i: piece(planes[1] * part + (cell + cores * i) % part + j, 1, place).start())
+        each(part // cores, lambda i: piece(planes[1] * part + part - cores * (i + 1), 1, place).start())
+        for j in range(1, cores):
+            each(part // cores, lambda i: piece(planes[1] * part + (cell + cores * (i + 1)) % part + j, 1, place).start())
 
     @pl.when(plane == 2)
     def _():
         tell(-part, 0)
         for j in range(cores):
             facing(j, 0)
-        for g, p in groups[1 : 2 * GB]:
-            ready(g, p)
+        for k in range(1, GB + 1):
+            ready(k)
         hear(0)
         others(0)
         hear(2)
@@ -195,37 +200,39 @@
         hear(1)
         tell(part, 0)
         send_plane(0, 0)
-        send_plane(0, 1)
+        each(part - cores, lambda i: piece(planes[0] * part + cores + (low + i) % (part - cores), 1, place).start())
         for j in range(cores):
             each(part // cores, lambda i: piece(planes[1] * part + (cell + cores * i) % part + j, 1, place).start())
+        each(cores, lambda i: piece(planes[0] * part + i, 1, place).start())
 
     @pl.when(plane == 3)
     def _():
         tell(-part, 2)
-        for g, p in groups[1 : 2 * GB]:
-            ready(g, p)
+        for k in range(1, GB + 1):
+            ready(k)
         hear(0)
         send_plane(1, 0)
         send_plane(0, 0)
-        send_plane(0, 1)
+        each(part - cores, lambda i: piece(planes[0] * part + cores + (low + i) % (part - cores), 1, place).start())
         for j in range(cores):
             each(part // cores, lambda i: piece(planes[1] * part + (cell + cores * i) % part + j, 1, place).start())
-
+        each(cores, lambda i: piece(planes[0] * part + i, 1, place).start())
+
+    ready(GB + 1)
     for g, p in groups[2 * GB :]:
-        ready(g, p)
         send_plane(p, g)
+    for copy in small:
+        copy.wait()
     swap = pltpu.make_async_remote_copy(
         src_ref=bw.at[1 - core],
         dst_ref=wfull.at[core],
-        send_sem=wsem.at[0],
-        recv_sem=wsem.at[1],
+        send_sem=lsem.at[2],
+        recv_sem=rsem.at[0],
         device_id={"sub": 1 - core},
         device_id_type=MESH,
     )
     swap.start()
 
-    for copy in small:
-        copy.wait()
     chosen = jnp.concatenate([sub[s : s + 1, :] for s in range(ns)], axis=1)
     picks = []
     for q in range(4):
@@ -289,21 +296,20 @@
         return pltpu.make_async_remote_copy(
             src_ref=esend,
             dst_ref=erecv.at[me],
-            send_sem=esem.at[0],
-            recv_sem=esem.at[1],
+            send_sem=lsem.at[3],
+            recv_sem=rsem.at[1],
             device_id=where(d),
             device_id_type=MESH,
         )
 
     def wait_for(g, p):
-        if p == 3:
-            mine[g].wait()
-        ref = slots(recv, g, p, part - int(p == 3))
+        if p == 2 and g == 0:
+            pltpu.make_async_copy(recv.at[:, me], recv.at[:, me], lsem.at[0]).wait()
+        ref = recv.at[g, pl.ds(0, 2 * part - 1)] if p == 2 else slots(recv, g, p)
         arrived(ref, ref, p, g).wait_recv()
 
     factor = 1.0 / (GB * pulses)
     for g in range(GB):
-        wait_for(g, 3)
         wait_for(g, 2)
         own, next_to = build(3, g), build(2, g)
         eacc[...] = beam(3, *own) + beam(2, *next_to)
@@ -370,8 +376,8 @@
     shared = pltpu.make_async_remote_copy(
         src_ref=reports,
         dst_ref=reports,
-        send_sem=esem.at[0],
-        recv_sem=esem.at[1],
+        send_sem=lsem.at[3],
+        recv_sem=rsem.at[1],
         device_id=where(device(2, 0)),
         device_id_type=MESH,
     )
@@ -429,11 +435,10 @@
             pltpu.VMEM((8, beams), F32),
             pltpu.VMEM((n, 8, beams), F32),
             dma((1,)),
-            dma((GB, 4)),
-            dma((GB, 4)),
+            dma((GB, 3)),
+            dma((GB + 2,)),
             dma((2,)),
-            dma((2,)),
-            dma((5,)),
+            dma((4,)),
             pltpu.SemaphoreType.REGULAR((3,)),
         ],
         compiler_params=pltpu.CompilerParams(collective_id=0, has_side_effects=True),

time: 33.9 us -> 33.4 us (0.985)
  Pallas kernels: 33.1 us -> 32.7 us
    pallas_call x1, Pallas kernels: 32.2 us -> 31.8 us  [body(): pl.pallas_call(functools.partial(kernel, dims), out_shape=(pltpu.VMEM((ns...]
where the time goes in v4:
time: 33.4 us; the launch traced here: 33.3 us
  Pallas kernels  32.7 us (98%)
  between operations  0.64 us (2%)
    pallas_call x1, Pallas kernels, body(): pl.pallas_call(functools.partial(kernel, dims), out_shape=(pltpu.VMEM((ns...  31.8 us
    pallas_call x1, Pallas kernels, body(): pl.pallas_call(store, out_shape=[jax.ShapeDtypeStruct(v.shape, F32) for v...  0.82 us

profile of v4, /device:TPU:0, one launch (start us, length us, event | category | flops | bytes accessed | tf_op | source)
XLA Modules:
  0.0 33.3 jit_solution(5175590240924497292)
XLA Ops:
  0.6 31.8 %shard_map.67 = (f32[8,64,128]{2,1,0:T(8,128)S(1)}, f32[2,256,128]{2,1,0:T(8,128)S(1)}, f32[1,128]{1,0:T(1,128)S(1)}) custom-call(f32[64,32,128]{2,1,0:T(8,128)} %bitcast.5, f32[2,8,2,64,64]{4,3,2,1,0:T(8,128)} %bw.1, s32[8,64]{1,0:T(8,128)} %bitcast.6, s32[2]{0:T(128)} %trn_in.1), custom_call_target="tpu_custom_call" | custom-call | tf_op jit(solution)/shard_map/pallas_call | solution.py:412
  32.5 0.8 %shard_map.68 = (f32[8,64,128]{2,1,0:T(8,128)}, f32[2,256,128]{2,1,0:T(8,128)}, f32[1,128]{1,0:T(1,128)}) custom-call(f32[8,64,128]{2,1,0:T(8,128)S(1)} %get-tuple-element.9.cov, f32[2,256,128]{2,1,0:T(8,128)S(1)} %get-tuple-element.10.filt, f32[1,128]{1,0:T(1,128)S(1)} %get-tuple-element.11.en), custom_call_target="tpu_custom_call" | custom-call | tf_op jit(solution)/shard_map/pallas_call | solution.py:452

commit v5 on v4

--- a/solution.py
+++ b/solution.py
@@ -159,8 +159,8 @@
         hear(1)
         others(0)
         hear(2)
+        send_plane(0, 1)
         send_plane(0, 0)
-        send_plane(0, 1)
         each(part // cores, lambda i: piece(planes[1] * part + part - cores * (i + 1), 1, place).start())
         for j in range(1, cores):
             each(part // cores, lambda i: piece(planes[1] * part + (cell + cores * (i + 1)) % part + j, 1, place).start())
@@ -214,9 +214,9 @@
         send_plane(1, 0)
         send_plane(0, 0)
         each(part - cores, lambda i: piece(planes[0] * part + cores + (low + i) % (part - cores), 1, place).start())
+        each(cores, lambda i: piece(planes[0] * part + i, 1, place).start())
         for j in range(cores):
             each(part // cores, lambda i: piece(planes[1] * part + (cell + cores * i) % part + j, 1, place).start())
-        each(cores, lambda i: piece(planes[0] * part + i, 1, place).start())
 
     ready(GB + 1)
     for g, p in groups[2 * GB :]:
@@ -327,10 +327,11 @@
         e_im = full[:beams, pulses:] - full[beams:, :pulses]
         power = e_re * e_re + e_im * e_im
         if g < GB - 1:
-            psum[...] = power if g == 0 else psum[...] + power
+            folded = jnp.sum(jnp.transpose(power).reshape(pulses // 8, 8, beams), axis=0)
+            psum[...] = folded if g == 0 else psum[...] + folded
         else:
-            across = jnp.transpose(psum[...] + power)
-            esum = jnp.sum(across.reshape(pulses // 8, 8, beams), axis=0)
+            across = jnp.transpose(power)
+            esum = psum[...] + jnp.sum(across.reshape(pulses // 8, 8, beams), axis=0)
             esend[...] = esum
             erecv[me] = esum
             for j in range(3):
@@ -387,7 +388,7 @@
 
 
 def store(cov, filt, en, cov_out, filt_out, en_out, sem):
-    pairs = ((cov, cov_out), (filt, filt_out), (en, en_out))
+    pairs = ((en, en_out), (filt, filt_out), (cov, cov_out))
     copies = [pltpu.make_async_copy(a, b, sem.at[i]) for i, (a, b) in enumerate(pairs)]
     for copy in copies:
         copy.start()
@@ -431,7 +432,7 @@
             pltpu.VMEM((2 * beams, 2 * pulses), F32),
             pltpu.VMEM((2, chans, 2 * pulses), BF16),
             pltpu.VMEM((GB, 2, beams, pulses), F32),
-            pltpu.VMEM((beams, pulses), F32),
+            pltpu.VMEM((8, beams), F32),
             pltpu.VMEM((8, beams), F32),
             pltpu.VMEM((n, 8, beams), F32),
             dma((1,)),

time: 33.4 us -> 33.4 us (level)
  no operation moved by 1% of the time
where the time goes in v5:
time: 33.4 us; the launch traced here: 33.3 us
  Pallas kernels  32.7 us (98%)
  between operations  0.64 us (2%)
    pallas_call x1, Pallas kernels, body(): pl.pallas_call(functools.partial(kernel, dims), out_shape=(pltpu.VMEM((ns...  31.8 us
    pallas_call x1, Pallas kernels, body(): pl.pallas_call(store, out_shape=[jax.ShapeDtypeStruct(v.shape, F32) for v...  0.82 us

profile of v5, /device:TPU:0, one launch (start us, length us, event | category | flops | bytes accessed | tf_op | source)
XLA Modules:
  0.0 33.3 jit_solution(9338039333748333024)
XLA Ops:
  0.6 31.8 %shard_map.67 = (f32[8,64,128]{2,1,0:T(8,128)S(1)}, f32[2,256,128]{2,1,0:T(8,128)S(1)}, f32[1,128]{1,0:T(1,128)S(1)}) custom-call(f32[64,32,128]{2,1,0:T(8,128)} %bitcast.5, f32[2,8,2,64,64]{4,3,2,1,0:T(8,128)} %bw.1, s32[8,64]{1,0:T(8,128)} %bitcast.6, s32[2]{0:T(128)} %trn_in.1), custom_call_target="tpu_custom_call" | custom-call | tf_op jit(solution)/shard_map/pallas_call | solution.py:413
  32.5 0.8 %shard_map.68 = (f32[8,64,128]{2,1,0:T(8,128)}, f32[2,256,128]{2,1,0:T(8,128)}, f32[1,128]{1,0:T(1,128)}) custom-call(f32[8,64,128]{2,1,0:T(8,128)S(1)} %get-tuple-element.9.cov, f32[2,256,128]{2,1,0:T(8,128)S(1)} %get-tuple-element.10.filt, f32[1,128]{1,0:T(1,128)S(1)} %get-tuple-element.11.en), custom_call_target="tpu_custom_call" | custom-call | tf_op jit(solution)/shard_map/pallas_call | solution.py:453

commit v6 on v4

--- a/solution.py
+++ b/solution.py
@@ -167,10 +167,10 @@
 
     @pl.when(plane == 1)
     def _():
-        tell(part, 0)
-        tell(-part, 0)
         for j in range(cores):
             facing(j, 0)
+        tell(-part, 0)
+        tell(part, 0)
         for k in range(1, GB + 1):
             ready(k)
         hear(0)

time: 33.4 us -> 33.4 us (level)
  no operation moved by 1% of the time
where the time goes in v6:
time: 33.4 us; the launch traced here: 33.3 us
  Pallas kernels  32.7 us (98%)
  between operations  0.64 us (2%)
    pallas_call x1, Pallas kernels, body(): pl.pallas_call(functools.partial(kernel, dims), out_shape=(pltpu.VMEM((ns...  31.8 us
    pallas_call x1, Pallas kernels, body(): pl.pallas_call(store, out_shape=[jax.ShapeDtypeStruct(v.shape, F32) for v...  0.82 us

profile of v6, /device:TPU:0, one launch (start us, length us, event | category | flops | bytes accessed | tf_op | source)
XLA Modules:
  0.0 33.3 jit_solution(12310148146294721140)
XLA Ops:
  0.6 31.8 %shard_map.67 = (f32[8,64,128]{2,1,0:T(8,128)S(1)}, f32[2,256,128]{2,1,0:T(8,128)S(1)}, f32[1,128]{1,0:T(1,128)S(1)}) custom-call(f32[64,32,128]{2,1,0:T(8,128)} %bitcast.5, f32[2,8,2,64,64]{4,3,2,1,0:T(8,128)} %bw.1, s32[8,64]{1,0:T(8,128)} %bitcast.6, s32[2]{0:T(128)} %trn_in.1), custom_call_target="tpu_custom_call" | custom-call | tf_op jit(solution)/shard_map/pallas_call | solution.py:412
  32.5 0.8 %shard_map.68 = (f32[8,64,128]{2,1,0:T(8,128)}, f32[2,256,128]{2,1,0:T(8,128)}, f32[1,128]{1,0:T(1,128)}) custom-call(f32[8,64,128]{2,1,0:T(8,128)S(1)} %get-tuple-element.9.cov, f32[2,256,128]{2,1,0:T(8,128)S(1)} %get-tuple-element.10.filt, f32[1,128]{1,0:T(1,128)S(1)} %get-tuple-element.11.en), custom_call_target="tpu_custom_call" | custom-call | tf_op jit(solution)/shard_map/pallas_call | solution.py:452
